TPU v7x, 32 devices: a whole 2x2x4 slice. The times are simulated.
32 devices in a mesh: pole: 2 (over y), prow: 4 (over z), pcol: 4 (over x, core).
Axes of the slice: x: 2, y: 2, z: 4, core: 2. Of those that a mesh axis runs over, the one named last changes fastest.
Arguments:
- ainv_anc: bfloat16 [2, 4096, 2048], P(None, ('pole', 'prow'), 'pcol'), parts along dimension 1, may hold values from -6 to 6
- panel: bfloat16 [2, 8, 1024, 256], P(None, 'pole', ('pcol', 'prow')), parts along dimension 1, may hold values from -6 to 6
- u_inv: bfloat16 [2, 8, 256, 256], P(None, 'pole'), parts along dimension 1, may hold values from -0.01171875 to 0.01171875
- k_inv: float32 [2, 8, 256, 256], P(None, ('pole', 'pcol')), parts along dimension 1, may hold values from -6 to 6
- structure: int32 [4, 4], replicated, may hold values from -1 to 7, as said below
Outputs:
- sel_inv: float32 [2, 4096, 1024], P(None, ('pole', 'prow'), 'pcol'), parts along dimension 1
- diag_inv: float32 [2, 8, 256, 256], P(None, ('pole', 'pcol')), parts along dimension 1
There are 2 independent parts, one for each index of `pole`. A program takes and returns all parts, laid end to end along the dimension named above; an argument that names none is the same for every part. Nothing has to cross between parts.
Inputs may be any that keep to these rules, and one draw needn't show every extreme that they name: `structure`: slots g * 1 to (g + 1) * 1 - 1 of row k hold distinct blocks of g * 2 to (g + 1) * 2 - 1 in rising order, followed by -1 for empty slots; each such group of each row holds at least one block, and for every g some row fills all 1 slots of group g.
All inputs are finite; a program needn't handle non-finite values.
Results may differ from a plain program's by a relative error of at most 0.005.
Values may be sent and summed in bfloat16 or wider, within the bound.
No kernel may reach another device: no remote copies, remote signals or barrier semaphores. Data moves between devices by JAX's collectives and lax.ppermute only.
A program may use at most 128 MiB of HBM per device.

v0:
```python
import jax
import jax.numpy as jnp
from jax import lax
from jax.sharding import PartitionSpec as P


def complex_quad(z_part, s_part):
    highest = lax.Precision.HIGHEST

    def single(left, right):
        return jnp.einsum("kra,rkb->kab", left, right, precision=highest)

    real = single(z_part[0], s_part[0]) - single(z_part[1], s_part[1])
    imag = single(z_part[0], s_part[1]) + single(z_part[1], s_part[0])
    return jnp.stack([real, imag])


def local(ainv_anc, panel, u_inv, k_inv, structure):
    block_width = u_inv.shape[-1]
    total_k = u_inv.shape[1]
    own_k = k_inv.shape[1]
    n_cols = lax.axis_size("pcol")
    row_here = lax.axis_index("prow")
    col_here = lax.axis_index("pcol")
    row_blocks = ainv_anc.shape[1] // block_width
    group_blocks = ainv_anc.shape[2] // block_width
    group_slots = structure.shape[1] // n_cols
    rows_all = row_blocks * block_width
    col_struct = lax.dynamic_slice_in_dim(structure, col_here * group_slots, group_slots, 1)
    slot_live = col_struct >= 0
    slot_pos = col_struct - col_here * group_blocks
    first_block = row_here * row_blocks
    target = first_block + jnp.arange(row_blocks, dtype=jnp.int32)
    rows_in = lax.all_gather(panel, "prow", axis=2, tiled=True)

    def single(left, right):
        return jnp.einsum("knb,kbc->knc", left, right, preferred_element_type=jnp.float32)

    real = single(rows_in[0], u_inv[0]) - single(rows_in[1], u_inv[1])
    imag = single(rows_in[0], u_inv[1]) + single(rows_in[1], u_inv[0])
    placed = jnp.stack([real, imag]).astype(jnp.bfloat16)
    placed = placed.reshape(2, total_k, group_slots, block_width, block_width)
    placed = jnp.where(slot_live[None, :, :, None, None], placed, jnp.zeros((), jnp.bfloat16))
    block_ids = jnp.arange(group_blocks, dtype=jnp.int32)
    pick_table = (slot_pos[:, :, None] == block_ids[None, None, :]).astype(jnp.bfloat16)
    ainv_blocks = ainv_anc.reshape(2, rows_all, group_blocks, block_width)

    def one_node(items):
        table_k, rows_k = items
        picked = jnp.einsum(
            "sg,cigw->cisw", table_k, ainv_blocks, preferred_element_type=jnp.float32
        )
        picked = picked.astype(jnp.bfloat16).reshape(2, rows_all, group_slots * block_width)
        right = rows_k.reshape(2, group_slots * block_width, block_width)
        real = jnp.dot(picked[0], right[0], preferred_element_type=jnp.float32) - jnp.dot(
            picked[1], right[1], preferred_element_type=jnp.float32
        )
        imag = jnp.dot(picked[0], right[1], preferred_element_type=jnp.float32) + jnp.dot(
            picked[1], right[0], preferred_element_type=jnp.float32
        )
        return jnp.stack([real, imag])

    per_node = lax.map(one_node, (pick_table, jnp.moveaxis(placed, 1, 0)))
    partial_value = jnp.transpose(per_node, (1, 2, 0, 3))
    row_table = (col_struct[:, None, :] == target[None, :, None]).astype(jnp.bfloat16)
    z_rows = jnp.einsum("kts,ckswb->cktwb", row_table, placed, preferred_element_type=jnp.float32)
    z_rows = z_rows.astype(jnp.bfloat16).reshape(2, total_k, rows_all, block_width)
    summed = lax.psum_scatter(
        partial_value.reshape(2, rows_all, total_k * block_width),
        "pcol",
        scatter_dimension=2,
        tiled=True,
    )
    own_struct = lax.dynamic_slice_in_dim(structure, col_here * own_k, own_k, 0)
    member = jnp.any(own_struct[:, :, None] == target[None, None, :], axis=1)
    selected = -summed.reshape(2, row_blocks, block_width, own_k, block_width)
    selected = jnp.where(member.T[None, :, None, :, None], selected, 0.0)
    sel_inv = selected.reshape(2, rows_all, own_k * block_width)
    received = lax.all_to_all(z_rows, "pcol", split_axis=1, concat_axis=1, tiled=True)
    z_own = (
        received.astype(jnp.float32).reshape(2, n_cols, own_k, rows_all, block_width).sum(axis=1)
    )
    quad_term = complex_quad(z_own, selected.reshape(2, rows_all, own_k, block_width))
    total_sum = lax.psum(quad_term, "prow")
    diag_inv = k_inv - total_sum
    return (sel_inv, diag_inv)


def solution(mesh):
    placed = (
        P(None, ("pole", "prow"), "pcol"),
        P(None, "pole", ("pcol", "prow"), None),
        P(None, "pole", None, None),
        P(None, ("pole", "pcol"), None, None),
        P(),
    )
    return jax.shard_map(
        local,
        mesh=mesh,
        in_specs=placed,
        out_specs=(P(None, ("pole", "prow"), "pcol"), P(None, ("pole", "pcol"), None, None)),
        check_vma=False,
    )
```

profile of v0, /device:TPU:0, one launch (start us, length us, event | category | flops | bytes accessed | tf_op | source)
XLA Modules:
  0.0 170.8 jit_solution(10218093751577018464)
XLA Ops:
  7.2 0.7 all-gather.2.cloned.1.call-update
  8.0 1.3 reshape.276
  9.3 0.9 compare_reduce_fusion
  10.2 0.9 dynamic-slice_reduce_fusion
  11.2 29.1 %all-gather.2.cloned.1.call-done = bf16[2,4,256,256]{3,2,1,0:T(8,128)(2,1)} async-done(((bf16[2,4,64,256]{3,2,1,0:T(8,128)(2,1)}), bf16[2,4,256,256]{3,2,1,0:T(8,128)(2,1)}) %all-gather.2.cloned.1.call-update) | async-done | bytes 1048592 | tf_op jit(solution)/shard_map/all_gather | solution.py:34
  40.3 1.6 fusion.13
  41.9 1.3 fusion.17
  43.3 0.3 fusion.9
  44.1 13.4 %while.10 = (s32[]{:T(128)}, f32[4,2,512,256]{3,2,1,0:T(8,128)}, bf16[4,1,2]{2,1,0:T(2,128)(2,1)S(1)}, bf16[2,512,2,256]{3,2,1,0:T(2,128)(2,1)S(1)}, bf16[4,2,1,256,256]{4,3,0,2,1:T(8,128)(2,1)S(1)}, /*index=5*/s32[]{:T(128)}) while((s32[]{:T(128)}, f32[4,2,512,256]{3,2,1,0:T(8,128)}, bf16[4,1,2]{2,1,0:T(2,128)(2,1)S(1)}, ...), condition=%wide.region_2.3_spmd, body=%wide.region_1.2_spmd.sunk | while | flops 270008320 | bytes 9962073 | solution.py:63
  44.1 1.2 fusion.42
  46.4 1.0 fusion.47
  47.4 1.2 fusion.42
  49.7 1.1 fusion.47
  50.8 1.2 fusion.42
  53.1 1.1 fusion.47
  54.2 1.2 fusion.42
  56.4 1.0 fusion.47
  57.5 4.8 %copy.21 = f32[4,2,64,8,256]{4,3,0,2,1:T(8,128)} copy(f32[4,2,64,8,256]{4,3,2,1,0:T(8,128)} %bitcast.135) | data formatting | bytes 8388608 | tf_op jit(solution)/shard_map/reshape | solution.py:69
  62.5 0.5 multiply_convert_fusion
  63.0 1.5 copy.17
  64.5 3.8 %all-to-all-start = ((bf16[2,4,512,256]{3,2,0,1:T(8,128)(2,1)}), bf16[2,4,512,256]{3,2,0,1:T(8,128)(2,1)S(1)}, u32[]{:S(2)}, u32[]{:S(2)}) async-start(bf16[2,4,512,256]{3,2,0,1:T(8,128)(2,1)} %copy.17), calls=%async_computation.1 | async-start | bytes 4194304 | tf_op jit(solution)/shard_map/all_to_all | solution.py:79
  68.3 0.7 dynamic-slice_bitcast_fusion.1
  69.2 36.9 %all-to-all-done = bf16[2,4,512,256]{3,2,0,1:T(8,128)(2,1)S(1)} async-done(((bf16[2,4,512,256]{3,2,0,1:T(8,128)(2,1)}), bf16[2,4,512,256]{3,2,0,1:T(8,128)(2,1)S(1)}, u32[]{:S(2)}, u32[]{:S(2)}) %all-to-all-start) | async-done | bytes 2097184 | tf_op jit(solution)/shard_map/all_to_all | solution.py:79
  106.4 11.5 %reduce-scatter.2.cloned.1.call-done = f32[2,512,256]{2,1,0:T(8,128)} async-done(((f32[2,512,1024]{2,1,0:T(8,128)}), f32[2,512,256]{2,1,0:T(8,128)}) %reduce-scatter.2.cloned.1.call-update) | async-done | bytes 1048592 | tf_op jit(solution)/shard_map/reduce_scatter | solution.py:68
  117.9 2.3 %fusion.26 = (f32[2,512,256]{2,1,0:T(8,128)S(1)}, f32[2,512,256]{2,1,0:T(8,128)}) fusion(f32[2,512,256]{2,1,0:T(8,128)} %reduce-scatter.2.cloned.1.call-done, pred[512]{0:T(512)(128)(4,1)S(1)} %broadcast_in_dim.53), kind=kLoop, calls=%fused_computation.59 | loop fusion | flops 524288 | bytes 3146240 | tf_op jit(solution)/shard_map/neg | solution.py:76
  120.5 1.0 fusion.19
  121.5 1.0 fusion.20
  122.5 1.0 fusion.10
  123.5 1.0 fusion.11
  124.5 0.8 pad_maximum_fusion
  125.4 37.0 %all-reduce.2.cloned.1.call-done = f32[2,1,256,256]{3,2,1,0:T(8,128)} async-done(((f32[2,1,256,256]{3,2,1,0:T(8,128)}), f32[2,1,256,256]{3,2,1,0:T(8,128)}) %all-reduce.2.cloned.1.call-update) | async-done | bytes 524304 | tf_op jit(solution)/shard_map/psum | solution.py:84
  162.4 1.9 %sub.26 = f32[2,1,256,256]{3,2,1,0:T(8,128)} subtract(f32[2,1,256,256]{3,2,1,0:T(8,128)S(1)} %copy-done.2, f32[2,1,256,256]{3,2,1,0:T(8,128)} %all-reduce.2.cloned.1.call-done) | non-fusion elementwise | flops 131072 | bytes 1572864 | tf_op jit(solution)/shard_map/sub | solution.py:85
  (48 shorter events, 5.7 us)
Async XLA Ops:
  7.2 34.7 %copy-start = (bf16[2,4,256,256]{3,2,1,0:T(8,128)(2,1)S(1)}, bf16[2,4,256,256]{3,2,1,0:T(8,128)(2,1)}, u32[]{:S(2)}) copy-start(bf16[2,4,256,256]{3,2,1,0:T(8,128)(2,1)} %param.9) | copy-start | bytes 3145732
  7.2 33.1 %all-gather.2.cloned.1.call-start = ((), (), s32[]{:S(2)}) async-start(), calls=%async_computation.2 | async-start | bytes 1310720 | tf_op jit(solution)/shard_map/all_gather | solution.py:34
  7.9 110.0 %reduce-scatter.2.cloned.1.call-start = ((), (), s32[]{:S(2)}) async-start(), calls=%async_computation.3 | async-start | bytes 5242880 | tf_op jit(solution)/shard_map/reduce_scatter | solution.py:68
  40.3 3.0 %copy-start.1 = (bf16[2,4,256,256]{3,2,1,0:T(8,128)(2,1)S(1)}, bf16[2,4,256,256]{3,2,1,0:T(8,128)(2,1)}, u32[]{:S(2)}) copy-start(bf16[2,4,256,256]{3,2,1,0:T(8,128)(2,1)} %all-gather.2.cloned.1.call-done) | copy-start | bytes 3145732
  64.5 41.6 %all-to-all-start = ((bf16[2,4,512,256]{3,2,0,1:T(8,128)(2,1)}), bf16[2,4,512,256]{3,2,0,1:T(8,128)(2,1)S(1)}, u32[]{:S(2)}, u32[]{:S(2)}) async-start(bf16[2,4,512,256]{3,2,0,1:T(8,128)(2,1)} %copy.17), calls=%async_computation.1 | async-start | bytes 4194304 | tf_op jit(solution)/shard_map/all_to_all | solution.py:79
  68.2 94.1 %all-reduce.2.cloned.1.call-start = ((), (), s32[]{:S(2)}) async-start(), calls=%async_computation.4 | async-start | bytes 1048576 | tf_op jit(solution)/shard_map/psum | solution.py:84
  120.4 41.9 %copy-start.2 = (f32[2,1,256,256]{3,2,1,0:T(8,128)S(1)}, f32[2,1,256,256]{3,2,1,0:T(8,128)}, u32[]{:S(2)}) copy-start(f32[2,1,256,256]{3,2,1,0:T(8,128)} %param.10) | copy-start | bytes 1572868
Sparse Core Ops, SparseCore 0:
  9.6 30.6 all-gather.1
  62.4 55.4 reduce-scatter.1
  125.5 36.8 all-reduce.1
where the time goes:
time: 171 us
  waiting for transfers between devices  115 us (67%)
  matrix products  16.1 us (9%)
  between operations  13.9 us (8%)
  other arithmetic  12.6 us (7%)
  local copies, waits for them, and re-layouts  8.88 us (5%)
  starting transfers between devices  3.88 us (2%)
    psum x1, waiting for transfers between devices, local(): total_sum = lax.psum(quad_term, 'prow')  37 us
    all_to_all x1, waiting for transfers between devices, local(): lax.all_to_all(z_rows, 'pcol', split_axis=1, concat_axis=1, tiled=True)  36.9 us
    all_gather x1, waiting for transfers between devices, local(): rows_in = lax.all_gather(panel, 'prow', axis=2, tiled=True)  29.1 us
    reduce_scatter x1, waiting for transfers between devices, local(): lax.psum_scatter(partial_value.reshape(2, rows_all, total_k * block_width...  11.5 us
    dot_general x4, matrix products, one_node(): jnp.einsum('sg,cigw->cisw', table_k, ainv_blocks, preferred_element_type=...  4.94 us
    reshape x1, local copies, waits for them, and re-layouts, local(): partial_value.reshape(2, rows_all, total_k * block_width)  4.76 us
    dynamic_update_slice x4, other arithmetic, local(): per_node = lax.map(one_node, (pick_table, jnp.moveaxis(placed, 1, 0)))  4.27 us
    dot_general x4, matrix products, single(): return jnp.einsum('kra,rkb->kab', left, right, precision=highest)  4.02 us
  transfers between devices with their start and end apart: 4, of which 4 were waited for; matrix products, arithmetic and copies ran while one was open for 4% of the time, Pallas kernels for 0%

commit v1 on v0

--- a/solution.py
+++ b/solution.py
@@ -16,6 +16,10 @@
 
 
 def local(ainv_anc, panel, u_inv, k_inv, structure):
+
+    def direct_column(shard_in):
+        return jnp.sum(lax.all_gather(shard_in, axis_name="prow"), axis=0)
+
     block_width = u_inv.shape[-1]
     total_k = u_inv.shape[1]
     own_k = k_inv.shape[1]
@@ -81,7 +85,7 @@
         received.astype(jnp.float32).reshape(2, n_cols, own_k, rows_all, block_width).sum(axis=1)
     )
     quad_term = complex_quad(z_own, selected.reshape(2, rows_all, own_k, block_width))
-    total_sum = lax.psum(quad_term, "prow")
+    total_sum = direct_column(quad_term)
     diag_inv = k_inv - total_sum
     return (sel_inv, diag_inv)
 

time: 171 us -> 179 us (1.047)
  waiting for transfers between devices: 115 us -> 122 us
    all_gather x0 -> x1, waiting for transfers between devices: none -> 44.1 us  [direct_column(): return jnp.sum(lax.all_gather(shard_in, axis_name='prow'), axis=0)]
    psum x1 -> x0, waiting for transfers between devices: 37 us -> none  [local(): total_sum = lax.psum(quad_term, 'prow')]
where the time goes in v1:
time: 179 us
  waiting for transfers between devices  122 us (68%)
  matrix products  16.1 us (9%)
  between operations  13.9 us (8%)
  other arithmetic  13.4 us (7%)
  local copies, waits for them, and re-layouts  8.88 us (5%)
  starting transfers between devices  3.88 us (2%)
    all_gather x1, waiting for transfers between devices, direct_column(): return jnp.sum(lax.all_gather(shard_in, axis_name='prow'), axis=0)  44.1 us
    all_to_all x1, waiting for transfers between devices, local(): lax.all_to_all(z_rows, 'pcol', split_axis=1, concat_axis=1, tiled=True)  36.9 us
    all_gather x1, waiting for transfers between devices, local(): rows_in = lax.all_gather(panel, 'prow', axis=2, tiled=True)  29.1 us
    reduce_scatter x1, waiting for transfers between devices, local(): lax.psum_scatter(partial_value.reshape(2, rows_all, total_k * block_width...  11.5 us
    dot_general x4, matrix products, one_node(): jnp.einsum('sg,cigw->cisw', table_k, ainv_blocks, preferred_element_type=...  4.94 us
    reshape x1, local copies, waits for them, and re-layouts, local(): partial_value.reshape(2, rows_all, total_k * block_width)  4.76 us
    dynamic_update_slice x4, other arithmetic, local(): per_node = lax.map(one_node, (pick_table, jnp.moveaxis(placed, 1, 0)))  4.27 us
    dot_general x4, matrix products, single(): return jnp.einsum('kra,rkb->kab', left, right, precision=highest)  4.02 us
  transfers between devices with their start and end apart: 4, of which 4 were waited for; matrix products, arithmetic and copies ran while one was open for 4% of the time, Pallas kernels for 0%

profile of v1, /device:TPU:0, one launch (start us, length us, event | category | flops | bytes accessed | tf_op | source)
XLA Modules:
  0.0 178.7 jit_solution(3301416027574723989)
XLA Ops:
  7.2 0.7 all-gather.4.cloned.1.call-update
  8.0 1.3 reshape.277
  9.3 0.9 compare_reduce_fusion
  10.2 0.9 dynamic-slice_reduce_fusion
  11.2 29.1 %all-gather.4.cloned.1.call-done = bf16[2,4,256,256]{3,2,1,0:T(8,128)(2,1)} async-done(((bf16[2,4,64,256]{3,2,1,0:T(8,128)(2,1)}), bf16[2,4,256,256]{3,2,1,0:T(8,128)(2,1)}) %all-gather.4.cloned.1.call-update) | async-done | bytes 1048592 | tf_op jit(solution)/shard_map/all_gather | solution.py:38
  40.3 1.6 fusion.13
  41.9 1.3 fusion.17
  44.1 13.4 %while.10 = (s32[]{:T(128)}, f32[4,2,512,256]{3,2,1,0:T(8,128)}, bf16[4,1,2]{2,1,0:T(2,128)(2,1)S(1)}, bf16[2,512,2,256]{3,2,1,0:T(2,128)(2,1)S(1)}, bf16[4,2,1,256,256]{4,3,0,2,1:T(8,128)(2,1)S(1)}, /*index=5*/s32[]{:T(128)}) while((s32[]{:T(128)}, f32[4,2,512,256]{3,2,1,0:T(8,128)}, bf16[4,1,2]{2,1,0:T(2,128)(2,1)S(1)}, ...), condition=%wide.region_2.3_spmd, body=%wide.region_1.2_spmd.sunk | while | flops 270008320 | bytes 9962073 | solution.py:67
  44.1 1.2 fusion.42
  46.4 1.0 fusion.47
  47.4 1.2 fusion.42
  49.7 1.1 fusion.47
  50.8 1.2 fusion.42
  53.1 1.1 fusion.47
  54.2 1.2 fusion.42
  56.4 1.0 fusion.47
  57.5 4.8 %copy.21 = f32[4,2,64,8,256]{4,3,0,2,1:T(8,128)} copy(f32[4,2,64,8,256]{4,3,2,1,0:T(8,128)} %bitcast.140) | data formatting | bytes 8388608 | tf_op jit(solution)/shard_map/reshape | solution.py:73
  62.5 0.5 multiply_convert_fusion
  63.0 1.5 copy.17
  64.5 3.8 %all-to-all-start = ((bf16[2,4,512,256]{3,2,0,1:T(8,128)(2,1)}), bf16[2,4,512,256]{3,2,0,1:T(8,128)(2,1)S(1)}, u32[]{:S(2)}, u32[]{:S(2)}) async-start(bf16[2,4,512,256]{3,2,0,1:T(8,128)(2,1)} %copy.17), calls=%async_computation.1 | async-start | bytes 4194304 | tf_op jit(solution)/shard_map/all_to_all | solution.py:83
  68.3 0.7 dynamic-slice_bitcast_fusion.1
  69.2 36.9 %all-to-all-done = bf16[2,4,512,256]{3,2,0,1:T(8,128)(2,1)S(1)} async-done(((bf16[2,4,512,256]{3,2,0,1:T(8,128)(2,1)}), bf16[2,4,512,256]{3,2,0,1:T(8,128)(2,1)S(1)}, u32[]{:S(2)}, u32[]{:S(2)}) %all-to-all-start) | async-done | bytes 2097184 | tf_op jit(solution)/shard_map/all_to_all | solution.py:83
  106.4 11.5 %reduce-scatter.2.cloned.1.call-done = f32[2,512,256]{2,1,0:T(8,128)} async-done(((f32[2,512,1024]{2,1,0:T(8,128)}), f32[2,512,256]{2,1,0:T(8,128)}) %reduce-scatter.2.cloned.1.call-update) | async-done | bytes 1048592 | tf_op jit(solution)/shard_map/reduce_scatter | solution.py:72
  117.9 2.3 %fusion.26 = (f32[2,512,256]{2,1,0:T(8,128)S(1)}, f32[2,512,256]{2,1,0:T(8,128)}) fusion(f32[2,512,256]{2,1,0:T(8,128)} %reduce-scatter.2.cloned.1.call-done, pred[512]{0:T(512)(128)(4,1)S(1)} %broadcast_in_dim.53), kind=kLoop, calls=%fused_computation.61 | loop fusion | flops 524288 | bytes 3146240 | tf_op jit(solution)/shard_map/neg | solution.py:80
  120.4 1.0 fusion.19
  121.5 1.0 fusion.20
  122.5 1.0 fusion.10
  123.5 1.0 fusion.11
  124.5 0.8 pad_maximum_fusion
  125.4 44.1 %all-gather.6.cloned.1.call-done = f32[8,1,256,256]{3,2,1,0:T(8,128)} async-done(((f32[2,1,256,256]{3,2,1,0:T(8,128)}), f32[8,1,256,256]{3,2,1,0:T(8,128)}) %all-gather.6.cloned.1.call-update) | async-done | bytes 2097168 | tf_op jit(solution)/shard_map/all_gather | solution.py:21
  169.5 1.8 bitcast_reduce_fusion
  171.3 0.9 bitcast_subtract_fusion
  (49 shorter events, 6.0 us)
Async XLA Ops:
  7.2 34.7 %copy-start = (bf16[2,4,256,256]{3,2,1,0:T(8,128)(2,1)S(1)}, bf16[2,4,256,256]{3,2,1,0:T(8,128)(2,1)}, u32[]{:S(2)}) copy-start(bf16[2,4,256,256]{3,2,1,0:T(8,128)(2,1)} %param.9) | copy-start | bytes 3145732
  7.2 33.1 %all-gather.4.cloned.1.call-start = ((), (), s32[]{:S(2)}) async-start(), calls=%async_computation.2 | async-start | bytes 1310720 | tf_op jit(solution)/shard_map/all_gather | solution.py:38
  7.9 110.0 %reduce-scatter.2.cloned.1.call-start = ((), (), s32[]{:S(2)}) async-start(), calls=%async_computation.3 | async-start | bytes 5242880 | tf_op jit(solution)/shard_map/reduce_scatter | solution.py:72
  40.3 3.0 %copy-start.1 = (bf16[2,4,256,256]{3,2,1,0:T(8,128)(2,1)S(1)}, bf16[2,4,256,256]{3,2,1,0:T(8,128)(2,1)}, u32[]{:S(2)}) copy-start(bf16[2,4,256,256]{3,2,1,0:T(8,128)(2,1)} %all-gather.4.cloned.1.call-done) | copy-start | bytes 3145732
  64.5 41.6 %all-to-all-start = ((bf16[2,4,512,256]{3,2,0,1:T(8,128)(2,1)}), bf16[2,4,512,256]{3,2,0,1:T(8,128)(2,1)S(1)}, u32[]{:S(2)}, u32[]{:S(2)}) async-start(bf16[2,4,512,256]{3,2,0,1:T(8,128)(2,1)} %copy.17), calls=%async_computation.1 | async-start | bytes 4194304 | tf_op jit(solution)/shard_map/all_to_all | solution.py:83
  68.2 101.3 %all-gather.6.cloned.1.call-start = ((), (), s32[]{:S(2)}) async-start(), calls=%async_computation.4 | async-start | bytes 2621440 | tf_op jit(solution)/shard_map/all_gather | solution.py:21
  121.5 49.8 %copy-start.2 = (f32[2,1,256,256]{3,2,1,0:T(8,128)S(1)}, f32[2,1,256,256]{3,2,1,0:T(8,128)}, u32[]{:S(2)}) copy-start(f32[2,1,256,256]{3,2,1,0:T(8,128)} %param.10) | copy-start | bytes 1572868
Sparse Core Ops, SparseCore 0:
  9.6 30.6 all-gather.3
  62.4 55.4 reduce-scatter.1
  125.5 43.9 all-gather.5
